TPU v7x, 32 devices: a whole 2x2x4 slice. The times are simulated.
32 devices in a mesh: dp: 4 (over y, x), expert: 4 (over z), tensor: 2 (over core).
Axes of the slice: x: 2, y: 2, z: 4, core: 2. Of those that a mesh axis runs over, the one named last changes fastest.
Arguments:
- out_grad: bfloat16 [2048, 2048], P(('dp', 'expert'), 'tensor'), may hold values from -6 to 6
- seq_ids: int32 [16, 128], P(('dp', 'expert')), may hold values from 0 to 3, never falling along the last dimension, each value on 1 to 64 neighbouring positions
- seq_weights: float32 [16, 4], P(('dp', 'expert')), may hold values from -1.5 to 1.5
- expert_ids: int32 [2048, 2], P(('dp', 'expert')), may hold values from 0 to 3, all different within a row; in each aligned block of 128 rows (0 to 127, 128 to 255, ...) at most 96 rows name the same one
- route_probs: bfloat16 [2048, 2], P(('dp', 'expert')), may hold values from 0.19921875 to 1
- down_weight: bfloat16 [4, 7168, 2048], P('expert', ('dp', 'tensor')), may hold values from -0.0625 to 0.0625
- gate_pre: bfloat16 [4, 7168, 1536], P('expert', ('dp', 'tensor')), may hold values from -6 to 6
- up_pre: bfloat16 [4, 7168, 1536], P('expert', ('dp', 'tensor')), may hold values from -6 to 6
Outputs:
- grad_gate: bfloat16 [4, 7168, 1536], P('expert', ('dp', 'tensor'))
- grad_up: bfloat16 [4, 7168, 1536], P('expert', ('dp', 'tensor'))
- grad_down: bfloat16 [4, 7168, 2048], P('expert', ('dp', 'tensor'))
- grad_probs: float32 [2048, 2], P(('dp', 'expert'))
Inputs may be any that keep to these rules, and one draw needn't show every extreme that they name: `expert_ids`: the two experts of a token differ. Among the 128 tokens of one shard no expert is named more than 96 times, and in every draw some expert is named exactly 96 times by the tokens of some shard. `seq_ids`: along a shard's row the ids never fall; each of the 4 ids names 1 to 64 tokens of the row, and one names exactly 64.
All inputs are finite; a program needn't handle non-finite values.
Results may differ from a plain program's by a relative error of at most 0.0064.
Values may be sent and summed in bfloat16 or wider, within the bound.
A program may use at most 128 MiB of HBM per device.

v0:
```python
import jax
import jax.numpy as jnp
from jax import lax
from jax.sharding import PartitionSpec as P


def silu_parts(pre_act):
    logistic = jax.nn.sigmoid(pre_act)
    return (pre_act * logistic, logistic * (1.0 + pre_act * (1.0 - logistic)))


def local(out_grad, seq_ids, seq_weights, expert_ids, route_probs, down_weight, gate_pre, up_pre):
    experts = lax.axis_size("expert")
    columns = lax.axis_size("dp")
    token_count = seq_ids.shape[1]
    capacity = gate_pre.shape[2] // (columns * experts)
    half_width = out_grad.shape[1]
    seq_count = seq_weights.shape[1]
    block_size = experts * capacity
    gate_local = gate_pre[0]
    up_local = up_pre[0]
    weight_local = down_weight[0]
    member = (seq_ids[0][:, None] == jnp.arange(seq_count, dtype=jnp.int32)[None, :]).astype(
        jnp.float32
    )
    weight_tok = jnp.sum(member * seq_weights[0][None, :], axis=1)
    scaled = (weight_tok[:, None] * out_grad.astype(jnp.float32)).astype(jnp.bfloat16)
    chosen = expert_ids.reshape(-1)
    onehot = (chosen[:, None] == jnp.arange(experts, dtype=jnp.int32)[None, :]).astype(jnp.int32)
    earlier = jnp.cumsum(onehot, axis=0) - onehot
    slot_index = chosen * capacity + jnp.sum(earlier * onehot, axis=1)
    send_rows = (
        jnp.zeros((block_size, half_width), jnp.bfloat16)
        .at[slot_index]
        .set(jnp.repeat(scaled, 2, axis=0))
    )
    send_probs = jnp.zeros((block_size,), jnp.bfloat16).at[slot_index].set(route_probs.reshape(-1))
    copies = jnp.tile(send_rows, (columns, 1))
    copy_probs = jnp.tile(send_probs, (columns,))
    arrived, arrived_probs = (
        lax.all_to_all(copies, ("dp", "expert"), split_axis=0, concat_axis=0, tiled=True),
        lax.all_to_all(copy_probs, ("dp", "expert"), split_axis=0, concat_axis=0, tiled=True),
    )
    gathered = lax.all_gather(arrived, "tensor", axis=1, tiled=True)
    gate_piece = gate_local.astype(jnp.float32)
    up_piece = up_local.astype(jnp.float32)
    activated, derivative = silu_parts(gate_piece)
    hidden = (activated * up_piece).astype(jnp.bfloat16)
    upstream = lax.dot_general(
        weight_local, gathered, (((1,), (1,)), ((), ())), preferred_element_type=jnp.float32
    )
    partial_value = jnp.sum(upstream * hidden.astype(jnp.float32), axis=0)
    grad_hidden = arrived_probs.astype(jnp.float32)[None, :] * upstream
    gate_out = (grad_hidden * up_piece * derivative).astype(jnp.bfloat16)
    up_out = (grad_hidden * activated).astype(jnp.bfloat16)
    weighted = (arrived_probs.astype(jnp.float32)[:, None] * gathered.astype(jnp.float32)).astype(
        jnp.bfloat16
    )
    grad_w = jnp.dot(hidden, weighted, preferred_element_type=jnp.float32)
    gate_acc = gate_out
    up_acc = up_out
    probe = partial_value
    grad_w, gate_acc, up_acc, probe = (grad_w, gate_acc, up_acc, probe)
    summed = lax.psum(probe, ("dp", "tensor"))
    own_totals = lax.dynamic_slice_in_dim(summed, lax.axis_index("dp") * block_size, block_size, 0)
    returned = lax.all_to_all(own_totals, "expert", split_axis=0, concat_axis=0, tiled=True)
    grad_probs = returned[slot_index].reshape(token_count, 2)
    return (gate_acc[None], up_acc[None], grad_w.astype(jnp.bfloat16)[None], grad_probs)


def solution(mesh):
    return jax.shard_map(
        local,
        mesh=mesh,
        in_specs=(
            P(("dp", "expert"), "tensor"),
            P(("dp", "expert"), None),
            P(("dp", "expert"), None),
            P(("dp", "expert"), None),
            P(("dp", "expert"), None),
            P("expert", ("dp", "tensor"), None),
            P("expert", ("dp", "tensor"), None),
            P("expert", ("dp", "tensor"), None),
        ),
        out_specs=(
            P("expert", ("dp", "tensor"), None),
            P("expert", ("dp", "tensor"), None),
            P("expert", ("dp", "tensor"), None),
            P(("dp", "expert"), None),
        ),
        check_vma=False,
    )
```

profile of v0, /device:TPU:0, one launch (start us, length us, event | category | flops | bytes accessed | tf_op | source)
XLA Modules:
  0.0 166.8 jit_solution(17966599329222551912)
XLA Ops:
  7.2 0.8 copy.39
  8.0 0.1 eq.44
  8.1 0.1 eq.40
  8.3 0.7 broadcast_multiply_fusion
  9.0 1.2 reduce-window.6
  10.3 0.1 copy.41
  10.6 0.1 copy.38
  10.7 0.1 mul.82
  10.8 0.8 select_reduce_fusion
  11.6 1.1 multiply_convert_fusion.5
  12.6 0.3 broadcast_in_dim.28
  12.9 0.2 reshape.128
  13.2 1.9 %scatter_custom_fusion.1 = bf16[384,1024]{1,0:T(8,128)(2,1)S(1)} fusion(s32[256]{0:T(256)S(1)} %bitcast.78, bf16[256,1024]{1,0:T(8,128)(2,1)S(1)} %reshape.128, bf16[]{:T(256)} %constant.8.clone.1), kind=kCustom, calls=%fused_computation.29 | custom fusion | bytes 786434 | tf_op jit(solution)/shard_map/scatter | solution.py:35
  15.1 0.4 tile.21
  15.5 80.9 %all_to_all.30 = bf16[16,96,1024]{2,1,0:T(8,128)(2,1)} all-to-all(bf16[16,96,1024]{2,1,0:T(8,128)(2,1)S(1)} %bitcast.76), channel_id=1, replica_groups=mesh['dp'=4,'expert'=4,'tensor'=2] {'dp','expert'}, dimensions={0} | all-to-all | bytes 6291456 | tf_op jit(solution)/shard_map/all_to_all | solution.py:41
  96.4 0.1 copy.43
  96.6 0.1 reshape.120
  96.7 2.2 %scatter_custom_fusion = bf16[384]{0:T(512)(128)(2,1)S(1)} fusion(s32[256]{0:T(256)S(1)} %bitcast.79, bf16[256]{0:T(256)(128)(2,1)S(1)} %reshape.120, bf16[]{:T(256)} %constant.8.clone.1), kind=kCustom, calls=%fused_computation.44 | custom fusion | bytes 770 | tf_op jit(solution)/shard_map/scatter | solution.py:37
  99.0 0.6 copy.44
  99.6 3.5 %all-to-all-start = ((bf16[16,96,1]{1,2,0:T(2,128)(2,1)}), bf16[16,96,1]{1,2,0:T(2,128)(2,1)S(1)}, u32[]{:S(2)}, u32[]{:S(2)}) async-start(bf16[16,96,1]{1,2,0:T(2,128)(2,1)} %copy.44), calls=%async_computation | async-start | bytes 16384 | tf_op jit(solution)/shard_map/all_to_all | solution.py:42
  103.1 7.2 %all-to-all-done = bf16[16,96,1]{1,2,0:T(2,128)(2,1)S(1)} async-done(((bf16[16,96,1]{1,2,0:T(2,128)(2,1)}), bf16[16,96,1]{1,2,0:T(2,128)(2,1)S(1)}, u32[]{:S(2)}, u32[]{:S(2)}) %all-to-all-start) | async-done | bytes 3104 | tf_op jit(solution)/shard_map/all_to_all | solution.py:42
  110.4 0.2 all-gather.2.cloned.1.call-done
  110.6 14.0 %fusion.10 = (f32[1536]{0:T(1024)S(1)}, bf16[1,896,1536]{2,1,0:T(8,128)(2,1)}, bf16[1,896,1536]{2,1,0:T(8,128)(2,1)}) fusion(bf16[1,896,1536]{2,1,0:T(8,128)(2,1)S(1)} %copy-done.1, bf16[1,896,1536]{2,1,0:T(8,128)(2,1)} %param.14, f32[1536]{0:T(1024)S(1)} %reshape.105, bf16[1536,2048]{1,0:T(8,128)(2,1)} %all-gather.2.cloned.1.call-done, ...), kind=kOutput, calls=%fused_computation.21 | convolution fusion | flops 5666044416 | bytes 20983808 | tf_op jit(solution)/shard_map/dot_general | solution.py:49
  124.5 14.6 %psum.7 = f32[1536]{0:T(1024)S(1)} all-reduce(f32[1536]{0:T(1024)S(1)} %get-tuple-element.20), channel_id=1, replica_groups=mesh['dp'=4,'expert'=4,'tensor'=2] {'dp','tensor'}, use_global_device_ids=true, to_apply=%region_7.8 | all-reduce | flops 1536 | bytes 12288 | tf_op jit(solution)/shard_map/psum | solution.py:64
  139.2 0.7 all_to_all.24
  139.9 4.6 %all-to-all-start.2 = ((f32[4,96,1]{1,2,0:T(1,128)}), f32[4,96,1]{1,2,0:T(1,128)S(1)}, u32[]{:S(2)}, u32[]{:S(2)}) async-start(f32[4,96,1]{1,2,0:T(1,128)} %bitcast.18), calls=%async_computation.2 | async-start | bytes 4096 | tf_op jit(solution)/shard_map/all_to_all | solution.py:66
  144.5 11.4 %convert_bitcast_fusion = bf16[1,896,2048]{2,1,0:T(8,128)(2,1)} fusion(bf16[1536,2048]{1,0:T(8,128)(2,1)} %all-gather.2.cloned.1.call-done, f32[1536]{0:T(1024)S(1)} %reshape.105, bf16[1,896,1536]{2,1,0:T(8,128)(2,1)S(1)} %copy-done.1, bf16[1,896,1536]{2,1,0:T(8,128)(2,1)} %param.14), kind=kOutput, calls=%fused_computation.25 | convolution fusion | flops 5659426816 | bytes 15472640 | tf_op jit(solution)/shard_map/dot_general | solution.py:59
  155.9 0.5 broadcast.90
  156.4 0.7 reduce.7
  157.2 1.9 %gather_fusion = f32[256]{0:T(256)S(1)} fusion(f32[384]{0:T(512)S(1)} %all_to_all.26, s32[1024]{0:T(1024)S(1)} %pad_clamp_fusion), kind=kCustom, calls=%fused_computation | custom fusion | bytes 3072 | tf_op jit(solution)/shard_map/gather | solution.py:67
  159.1 0.1 reshape.104
  159.3 0.6 copy.46
  (22 shorter events, 0.8 us)
Async XLA Ops:
  7.2 103.4 %all-gather.2.cloned.1.call-start = ((), (), s32[]{:S(2)}) async-start(), calls=%async_computation.3 | async-start | bytes 9437184 | tf_op jit(solution)/shard_map/all_gather | solution.py:44
  15.5 80.9 %copy-start = (bf16[128,2]{0,1:T(2,128)(2,1)S(1)}, bf16[128,2]{0,1:T(2,128)(2,1)}, u32[]{:S(2)}) copy-start(bf16[128,2]{0,1:T(2,128)(2,1)} %param.12) | copy-start | bytes 1540
  15.5 95.1 %copy-start.1 = (bf16[1,896,1536]{2,1,0:T(8,128)(2,1)S(1)}, bf16[1,896,1536]{2,1,0:T(8,128)(2,1)}, u32[]{:S(2)}) copy-start(bf16[1,896,1536]{2,1,0:T(8,128)(2,1)} %param.15) | copy-start | bytes 8257540
  99.6 10.7 %all-to-all-start = ((bf16[16,96,1]{1,2,0:T(2,128)(2,1)}), bf16[16,96,1]{1,2,0:T(2,128)(2,1)S(1)}, u32[]{:S(2)}, u32[]{:S(2)}) async-start(bf16[16,96,1]{1,2,0:T(2,128)(2,1)} %copy.44), calls=%async_computation | async-start | bytes 16384 | tf_op jit(solution)/shard_map/all_to_all | solution.py:42
  139.9 16.0 %all-to-all-start.2 = ((f32[4,96,1]{1,2,0:T(1,128)}), f32[4,96,1]{1,2,0:T(1,128)S(1)}, u32[]{:S(2)}, u32[]{:S(2)}) async-start(f32[4,96,1]{1,2,0:T(1,128)} %bitcast.18), calls=%async_computation.2 | async-start | bytes 4096 | tf_op jit(solution)/shard_map/all_to_all | solution.py:66
Sparse Core Ops, SparseCore 0:
  96.5 13.9 all-gather.1
where the time goes:
time: 167 us
  blocking collectives  95.4 us (57%)
  matrix products  25.4 us (15%)
  between operations  14.2 us (9%)
  local copies, waits for them, and re-layouts  11.7 us (7%)
  starting transfers between devices  8.11 us (5%)
  waiting for transfers between devices  7.37 us (4%)
  other arithmetic  4.55 us (3%)
    all_to_all x1, blocking collectives, local(): lax.all_to_all(copies, ('dp', 'expert'), split_axis=0, concat_axis=0, til...  80.9 us
    psum x1, blocking collectives, local(): summed = lax.psum(probe, ('dp', 'tensor'))  14.6 us
    dot_general x1, matrix products, local(): lax.dot_general(weight_local, gathered, (((1,), (1,)), ((), ())), preferr...  14 us
    dot_general x1, matrix products, local(): grad_w = jnp.dot(hidden, weighted, preferred_element_type=jnp.float32)  11.4 us
    all_to_all x1, waiting for transfers between devices, local(): lax.all_to_all(copy_probs, ('dp', 'expert'), split_axis=0, concat_axis=0,...  7.16 us
    all_to_all x1, starting transfers between devices, local(): lax.all_to_all(own_totals, 'expert', split_axis=0, concat_axis=0, tiled=T...  4.59 us
    all_to_all x1, starting transfers between devices, local(): lax.all_to_all(copy_probs, ('dp', 'expert'), split_axis=0, concat_axis=0,...  3.48 us
  transfers between devices with their start and end apart: 3, of which 2 were waited for; matrix products, arithmetic and copies ran while one was open for 9% of the time, Pallas kernels for 0%

commit v1 on v0

v1 whole, which is shorter than its diff:
```python
import functools

import jax
import jax.numpy as jnp
from jax import lax
from jax.experimental import pallas as pl
from jax.experimental.pallas import tpu as pltpu
from jax.sharding import PartitionSpec as P

MESH = pl.DeviceIdType.MESH
LANES = 128
SUBLANES = 8


def silu_parts(pre_act):
    logistic = jax.nn.sigmoid(pre_act)
    return (pre_act * logistic, logistic * (1.0 + pre_act * (1.0 - logistic)))


def flip(index, mask):
    bit = 1
    while bit <= mask:
        if mask & bit:
            index = index + bit * (1 - 2 * lax.rem(lax.div(index, bit), 2))
        bit *= 2
    return index


class Copies:
    def __init__(self, send_sem, recv_sem):
        self.send_sem, self.recv_sem, self.made = send_sem, recv_sem, []

    def start(self, src, dst, device):
        at = len(self.made)
        copy = pltpu.make_async_remote_copy(
            src_ref=src,
            dst_ref=dst,
            send_sem=self.send_sem.at[at],
            recv_sem=self.recv_sem.at[at],
            device_id=device,
            device_id_type=MESH,
        )
        copy.start()
        self.made.append(copy)
        return copy


def greet(peers):
    barrier = pltpu.get_barrier_semaphore()
    for peer in peers:
        pl.semaphore_signal(barrier, inc=1, device_id=peer, device_id_type=MESH)
    pl.semaphore_wait(barrier, len(peers))


def copy_count(columns, experts, cores):
    if columns == 4:
        per_block = 6 + 7 * (cores - 1)
        return (experts - 1) * 2 + (columns - 1) + experts * per_block
    return (experts - 1) * 2 + (columns - 1) * 2 + columns * (cores - 1)


def gather_kernel(
    columns, experts, cores, rows_ref, probs_ref, out_ref, probs_out, send_sem, recv_sem
):
    d, e, t = lax.axis_index("dp"), lax.axis_index("expert"), lax.axis_index("tensor")
    half = rows_ref.shape[2]
    peers = (
        [(d, flip(e, k), t) for k in range(1, experts)]
        + [(flip(d, m), e, t) for m in range(1, columns)]
        + [(d, e, flip(t, f)) for f in range(1, cores)]
    )
    greet(peers)
    copies = Copies(send_sem, recv_sem)
    base = pl.multiple_of(t * half, half)
    mine = pl.ds(base, half)
    along, small = [None], [None]
    for k in range(1, experts):
        to = (d, flip(e, k), t)
        along.append(copies.start(rows_ref.at[flip(e, k)], out_ref.at[d, e, :, mine], to))
        small.append(copies.start(probs_ref.at[flip(e, k)], probs_out.at[d, e], to))

    def to_cores(src, dst):
        return [copies.start(src, dst, (d, e, flip(t, f))) for f in range(1, cores)]

    last = []
    if columns == 4:
        piece = half // 2
        cuts = [pl.ds(pl.multiple_of(base + p * piece, piece), piece) for p in range(2)]
        sent = {}

        def spread(k):
            origin = flip(e, k)
            if k > 0:
                along[k].wait_recv()
            for m, order in ((1, (0, 1)), (2, (1, 0))):
                for p in order:
                    here = out_ref.at[d, origin, :, cuts[p]]
                    src = rows_ref.at[e, :, pl.ds(p * piece, piece)] if k == 0 else here
                    sent[k, m, p] = copies.start(src, here, (flip(d, m), e, t))
            whole = out_ref.at[d, origin, :, mine]
            last.extend(to_cores(rows_ref.at[e] if k == 0 else whole, whole))

        def forward(k):
            origin = flip(e, k)
            for m, p in ((1, 0), (2, 1)):
                sent[k, m, p].wait_recv()
                block = out_ref.at[flip(d, m), origin, :, cuts[p]]
                sent[k, 3, p] = copies.start(block, block, (flip(d, 3 - m), e, t))
                last.extend(to_cores(block, block))
            for m, p in ((1, 1), (2, 0)):
                sent[k, m, p].wait_recv()
                block = out_ref.at[flip(d, m), origin, :, cuts[p]]
                last.extend(to_cores(block, block))

        def finish(k):
            for p in range(2):
                sent[k, 3, p].wait_recv()
                block = out_ref.at[flip(d, 3), flip(e, k), :, cuts[p]]
                last.extend(to_cores(block, block))

        spread(0)
        out_ref[d, e, :, mine] = rows_ref[e]
        probs_out[d, e] = probs_ref[e]
        for k in range(1, experts):
            spread(k)
            forward(k - 1)
            if k > 1:
                finish(k - 2)
        forward(experts - 1)
        if experts > 1:
            finish(experts - 2)
        finish(experts - 1)
    else:
        out_ref[d, e, :, mine] = rows_ref[e]
        probs_out[d, e] = probs_ref[e]
        for k in range(1, experts):
            along[k].wait_recv()
        group = out_ref.at[d, :, :, mine]
        spreads = [copies.start(group, group, (flip(d, m), e, t)) for m in range(1, columns)]
        last.extend(to_cores(group, group))
        for m in range(1, columns):
            spreads[m - 1].wait_recv()
            block = out_ref.at[flip(d, m), :, :, mine]
            last.extend(to_cores(block, block))
    for k in range(1, experts):
        small[k].wait_recv()
    group = probs_out.at[d]
    for m in range(1, columns):
        last.append(copies.start(group, group, (flip(d, m), e, t)))
    for copy in last:
        copy.wait_recv()
    for copy in copies.made:
        copy.wait_send()


def probe_kernel(columns, experts, cores, part_ref, out_ref, first, total, second, send_sem, recv_sem):
    d, e, t = lax.axis_index("dp"), lax.axis_index("expert"), lax.axis_index("tensor")
    others = [(m, f) for m in range(columns) for f in range(cores) if m or f]
    greet(
        [(flip(d, m), e, flip(t, f)) for m, f in others]
        + [(d, flip(e, k), t) for k in range(1, experts)]
    )
    copies = Copies(send_sem, recv_sem)
    for at, (m, f) in enumerate(others):
        to = (flip(d, m), e, flip(t, f))
        copies.start(part_ref.at[flip(d, m)], first.at[at], to)
    acc = part_ref[d]
    for at in range(len(others)):
        copies.made[at].wait_recv()
        acc = acc + first[at]
    total[...] = acc
    backs = [copies.start(total, second.at[k - 1], (d, flip(e, k), t)) for k in range(1, experts)]
    out_ref[...] = jnp.zeros_like(out_ref)
    out_ref[pl.ds(e, 1), :] = total[pl.ds(e, 1), :]
    for k in range(1, experts):
        backs[k - 1].wait_recv()
        out_ref[pl.ds(flip(e, k), 1), :] = second[k - 1, pl.ds(e, 1), :]
    for copy in copies.made:
        copy.wait_send()


def local(out_grad, seq_ids, seq_weights, expert_ids, route_probs, down_weight, gate_pre, up_pre):
    experts = lax.axis_size("expert")
    columns = lax.axis_size("dp")
    cores = lax.axis_size("tensor")
    token_count = seq_ids.shape[1]
    slots = gate_pre.shape[2]
    capacity = slots // (columns * experts)
    half_width = out_grad.shape[1]
    width = half_width * cores
    seq_count = seq_weights.shape[1]
    block_size = experts * capacity
    padded = -(-capacity // LANES) * LANES
    depth = -(-experts // SUBLANES) * SUBLANES
    gate_local = gate_pre[0]
    up_local = up_pre[0]
    weight_local = down_weight[0]
    member = (seq_ids[0][:, None] == jnp.arange(seq_count, dtype=jnp.int32)[None, :]).astype(
        jnp.float32
    )
    weight_tok = jnp.sum(member * seq_weights[0][None, :], axis=1)
    scaled = (weight_tok[:, None] * out_grad.astype(jnp.float32)).astype(jnp.bfloat16)
    chosen = expert_ids.reshape(-1)
    pairs = chosen.shape[0]
    onehot = chosen[:, None] == jnp.arange(experts, dtype=jnp.int32)[None, :]
    rank = jnp.arange(pairs, dtype=jnp.int32)
    lower = (rank[None, :] < rank[:, None]).astype(jnp.bfloat16)
    earlier = jnp.dot(lower, onehot.astype(jnp.bfloat16), preferred_element_type=jnp.float32)
    position = jnp.sum(jnp.where(onehot, earlier, 0.0), axis=1).astype(jnp.int32)
    slot_index = chosen * capacity + position
    filled = slot_index[None, :] == jnp.arange(block_size, dtype=jnp.int32)[:, None]
    send_probs = jnp.sum(
        jnp.where(filled, route_probs.reshape(-1).astype(jnp.float32)[None, :], 0.0), axis=1
    )
    by_token = slot_index.reshape(token_count, 2)
    every = jnp.arange(block_size, dtype=jnp.int32)[:, None]
    picks = ((by_token[:, 0][None, :] == every) | (by_token[:, 1][None, :] == every)).astype(
        jnp.bfloat16
    )
    send_rows = jnp.dot(picks, scaled, preferred_element_type=jnp.float32).astype(jnp.bfloat16)
    prob_tile = jnp.zeros((experts, SUBLANES, padded), jnp.float32)
    prob_tile = prob_tile + jnp.pad(
        send_probs.reshape(experts, 1, capacity), ((0, 0), (0, 0), (0, padded - capacity))
    )
    amount = copy_count(columns, experts, cores)
    gathered, probs_all = pl.pallas_call(
        functools.partial(gather_kernel, columns, experts, cores),
        out_shape=(
            jax.ShapeDtypeStruct((columns, experts, capacity, width), jnp.bfloat16),
            jax.ShapeDtypeStruct((columns, experts, SUBLANES, padded), jnp.float32),
        ),
        in_specs=[pl.BlockSpec(memory_space=pltpu.VMEM)] * 2,
        out_specs=[pl.BlockSpec(memory_space=pltpu.VMEM)] * 2,
        scratch_shapes=[pltpu.SemaphoreType.DMA((amount,)), pltpu.SemaphoreType.DMA((amount,))],
        compiler_params=pltpu.CompilerParams(
            collective_id=0, has_side_effects=True, vmem_limit_bytes=40 * 1024 * 1024
        ),
        name="gather",
    )(send_rows.reshape(experts, capacity, half_width), prob_tile)
    gathered = gathered.reshape(slots, width)
    arrived_probs = probs_all[:, :, 0, :capacity].reshape(slots)

    gate_piece = gate_local.astype(jnp.float32)
    up_piece = up_local.astype(jnp.float32)
    activated, derivative = silu_parts(gate_piece)
    hidden = (activated * up_piece).astype(jnp.bfloat16)
    upstream = lax.dot_general(
        weight_local, gathered, (((1,), (1,)), ((), ())), preferred_element_type=jnp.float32
    )
    partial_value = jnp.sum(upstream * hidden.astype(jnp.float32), axis=0)
    grad_hidden = arrived_probs[None, :] * upstream
    gate_out = (grad_hidden * up_piece * derivative).astype(jnp.bfloat16)
    up_out = (grad_hidden * activated).astype(jnp.bfloat16)
    weighted = (arrived_probs[:, None] * gathered.astype(jnp.float32)).astype(jnp.bfloat16)
    grad_w = jnp.dot(hidden, weighted, preferred_element_type=jnp.float32).astype(jnp.bfloat16)

    parts = jnp.pad(
        partial_value.reshape(columns, experts, capacity),
        ((0, 0), (0, depth - experts), (0, padded - capacity)),
    )
    firsts = columns * cores - 1
    number = firsts + experts - 1
    totals = pl.pallas_call(
        functools.partial(probe_kernel, columns, experts, cores),
        out_shape=jax.ShapeDtypeStruct((depth, padded), jnp.float32),
        in_specs=[pl.BlockSpec(memory_space=pltpu.VMEM)],
        out_specs=pl.BlockSpec(memory_space=pltpu.VMEM),
        scratch_shapes=[
            pltpu.VMEM((firsts, depth, padded), jnp.float32),
            pltpu.VMEM((depth, padded), jnp.float32),
            pltpu.VMEM((experts - 1, depth, padded), jnp.float32),
            pltpu.SemaphoreType.DMA((number,)),
            pltpu.SemaphoreType.DMA((number,)),
        ],
        compiler_params=pltpu.CompilerParams(collective_id=1, has_side_effects=True),
        name="probe",
    )(parts)
    returned = totals[:experts, :capacity].reshape(-1)
    grad_probs = jnp.sum(jnp.where(filled, returned[:, None], 0.0), axis=0).reshape(token_count, 2)
    return (gate_out[None], up_out[None], grad_w[None], grad_probs)


def solution(mesh):
    return jax.shard_map(
        local,
        mesh=mesh,
        in_specs=(
            P(("dp", "expert"), "tensor"),
            P(("dp", "expert"), None),
            P(("dp", "expert"), None),
            P(("dp", "expert"), None),
            P(("dp", "expert"), None),
            P("expert", ("dp", "tensor"), None),
            P("expert", ("dp", "tensor"), None),
            P("expert", ("dp", "tensor"), None),
        ),
        out_specs=(
            P("expert", ("dp", "tensor"), None),
            P("expert", ("dp", "tensor"), None),
            P("expert", ("dp", "tensor"), None),
            P(("dp", "expert"), None),
        ),
        check_vma=False,
    )
```

time: 167 us -> 91.3 us (0.55)
  blocking collectives: 95.4 us -> 0 us
  Pallas kernels: 0 us -> 52.7 us
  between operations: 14.2 us -> 0.73 us
  starting transfers between devices: 8.11 us -> 0 us
  waiting for transfers between devices: 7.37 us -> 0 us
  local copies, waits for them, and re-layouts: 11.7 us -> 7.53 us
    all_to_all x1 -> x0, blocking collectives: 80.9 us -> none  [local(): lax.all_to_all(copies, ('dp', 'expert'), split_axis=0, concat_axis=0, til...]
    pallas_call x0 -> x2, Pallas kernels: none -> 52.7 us  [the longest x1 42.5 us: local(): pl.pallas_call(functools.partial(gather_kernel, columns, experts, cores),...]
    psum x1 -> x0, blocking collectives: 14.6 us -> none  [local(): summed = lax.psum(probe, ('dp', 'tensor'))]
    all_to_all x2 -> x0, starting transfers between devices: 8.08 us -> none  [the longest x1 4.59 us: local(): lax.all_to_all(own_totals, 'expert', split_axis=0, concat_axis=0, tiled=T...]
    all_to_all x2 -> x0, waiting for transfers between devices: 7.17 us -> none  [the longest x1 7.16 us: local(): lax.all_to_all(copy_probs, ('dp', 'expert'), split_axis=0, concat_axis=0,...]
    scatter x2 -> x0, local copies, waits for them, and re-layouts: 4.07 us -> none  [the longest x1 2.16 us: local(): jnp.zeros((block_size,), jnp.bfloat16).at[slot_index]]
    convert_element_type x3 -> x2, other arithmetic: 1.09 us -> 4.02 us  [the longest x1 4.01 us: local(): (arrived_probs[:, None] * gathered.astype(jnp.float32)).astype(jnp.bfloat16)]
    unnamed x7 -> x8, local copies, waits for them, and re-layouts: 1.57 us -> 4.47 us
  transfers between devices with their start and end apart: 3 -> 0, of which waited for: 2 -> 0; matrix products, arithmetic and copies ran while one was open for 9% -> 0% of each run, Pallas kernels for 0% -> 0%
where the time goes in v1:
time: 91.3 us; the launch traced here: 91 us
  Pallas kernels  52.7 us (58%)
  matrix products  24.2 us (27%)
  local copies, waits for them, and re-layouts  7.53 us (8%)
  other arithmetic  5.77 us (6%)
    pallas_call x1, Pallas kernels, local(): pl.pallas_call(functools.partial(gather_kernel, columns, experts, cores),...  42.5 us
    dot_general x1, matrix products, local(): lax.dot_general(weight_local, gathered, (((1,), (1,)), ((), ())), preferr...  14.8 us
    pallas_call x1, Pallas kernels, local(): pl.pallas_call(functools.partial(probe_kernel, columns, experts, cores),...  10.1 us
    dot_general x1, matrix products, local(): jnp.dot(hidden, weighted, preferred_element_type=jnp.float32)  7.86 us
    unnamed x8, local copies, waits for them, and re-layouts  4.47 us
    convert_element_type x1, other arithmetic, local(): (arrived_probs[:, None] * gathered.astype(jnp.float32)).astype(jnp.bfloat16)  4.01 us

profile of v1, /device:TPU:0, one launch (start us, length us, event | category | flops | bytes accessed | tf_op | source)
XLA Modules:
  0.0 91.0 jit_solution(17994490287473978395)
XLA Ops:
  0.6 0.8 select_reduce_fusion.2
  1.4 0.8 copy.29
  2.2 0.1 reshape.68
  2.3 0.8 copy.27
  3.1 0.1 eq.73
  3.2 0.2 fusion.24
  3.5 0.1 select_reduce_fusion.1
  3.6 0.1 reshape.64
  3.7 0.1 convert_element_type.87
  3.9 0.1 copy.28
  3.9 0.7 multiply_add_fusion.1
  4.6 1.4 %convolution_convert_fusion = bf16[384,1024]{1,0:T(8,128)(2,1)S(1)} fusion(bf16[128,1024]{1,0:T(8,128)(2,1)} %param.8, f32[128]{0:T(128)S(1)} %select_reduce_fusion.2, s32[128]{0:T(128)S(1)} %get-tuple-element.30, s32[128]{0:T(128)S(1)} %get-tuple-element.29), kind=kOutput, calls=%fused_computation.33 | convolution fusion | flops 101597184 | bytes 1050112 | tf_op jit(solution)/shard_map/dot_general | solution.py:220
  6.0 42.5 %gather.1 = (bf16[4,4,96,2048]{3,2,1,0:T(8,128)(2,1)S(1)}, f32[4,4,8,128]{3,2,1,0:T(8,128)S(1)}) custom-call(bf16[4,96,1024]{2,1,0:T(8,128)(2,1)S(1)} %bitcast.88, f32[4,8,128]{2,1,0:T(8,128)S(1)} %add.33.probs_ref), custom_call_target="tpu_custom_call" | custom-call | tf_op jit(solution)/shard_map/gather/pallas_call | solution.py:226
  48.6 0.0 copy-start
  48.6 2.7 %copy-done = bf16[4,4,96,2048]{3,2,1,0:T(8,128)(2,1)} copy-done((bf16[4,4,96,2048]{3,2,1,0:T(8,128)(2,1)}, bf16[4,4,96,2048]{3,2,1,0:T(8,128)(2,1)S(1)}, u32[]{:S(2)}) %copy-start) | copy-done | bytes 6291480
  51.3 0.1 mul.93
  51.3 14.8 %fusion.17 = (f32[1536]{0:T(1024)S(1)}, bf16[1,896,1536]{2,1,0:T(8,128)(2,1)}, bf16[1,896,1536]{2,1,0:T(8,128)(2,1)}) fusion(bf16[1,896,1536]{2,1,0:T(8,128)(2,1)} %param.15, bf16[1,896,1536]{2,1,0:T(8,128)(2,1)} %param.14, f32[1536]{0:T(1024)S(1)} %mul.93, bf16[1536,2048]{1,0:T(8,128)(2,1)} %bitcast.87, bf16[1,896,2048]{2,1,0:T(8,128)(2,1)} %param.13), kind=kOutput, calls=%fused_computation.25 | convolution fusion | flops 5666044416 | bytes 20983808 | tf_op jit(solution)/shard_map/dot_general | solution.py:247
  66.1 0.1 reshape.66
  66.2 0.6 pad.9.part_ref
  66.8 10.1 %probe.1 = f32[8,128]{1,0:T(8,128)} custom-call(f32[4,8,128]{2,1,0:T(8,128)} %pad.9.part_ref), custom_call_target="tpu_custom_call" | custom-call | tf_op jit(solution)/shard_map/probe/pallas_call | solution.py:263
  77.0 0.7 slice.15
  77.7 0.1 broadcast_in_dim.52
  77.8 0.1 select_reduce_fusion
  77.9 0.1 reshape.67
  78.0 0.6 copy.30
  78.7 0.0 copy-start.1
  78.7 0.0 copy-start.2
  78.7 4.0 %multiply_convert_fusion = bf16[4,4,96,2048]{3,2,1,0:T(8,128)(2,1)S(1)} fusion(bf16[4,4,96,2048]{3,2,1,0:T(8,128)(2,1)} %copy-done, f32[4,4,96]{2,1,0:T(4,128)S(1)} %bitcast.90), kind=kLoop, calls=%fused_computation | loop fusion | flops 9437184 | bytes 12589056 | tf_op jit(solution)/shard_map/convert_element_type | solution.py:254
  82.7 0.0 copy-done.1
  82.7 0.4 copy-done.2
  83.1 7.9 %convert_bitcast_fusion.2 = bf16[1,896,2048]{2,1,0:T(8,128)(2,1)} fusion(bf16[1536,2048]{1,0:T(8,128)(2,1)S(1)} %bitcast.89, bf16[1,896,1536]{2,1,0:T(8,128)(2,1)S(1)} %copy-done.1, bf16[1,896,1536]{2,1,0:T(8,128)(2,1)S(1)} %copy-done.2), kind=kOutput, calls=%fused_computation.29 | convolution fusion | flops 5649989632 | bytes 15466496 | tf_op jit(solution)/shard_map/dot_general | solution.py:255
  (6 shorter events, 0.1 us)
Async XLA Ops:
  48.6 2.7 %copy-start = (bf16[4,4,96,2048]{3,2,1,0:T(8,128)(2,1)}, bf16[4,4,96,2048]{3,2,1,0:T(8,128)(2,1)S(1)}, u32[]{:S(2)}) copy-start(bf16[4,4,96,2048]{3,2,1,0:T(8,128)(2,1)S(1)} %get-tuple-element.7) | copy-start | bytes 18874372
  78.7 4.0 %copy-start.1 = (bf16[1,896,1536]{2,1,0:T(8,128)(2,1)S(1)}, bf16[1,896,1536]{2,1,0:T(8,128)(2,1)}, u32[]{:S(2)}) copy-start(bf16[1,896,1536]{2,1,0:T(8,128)(2,1)} %param.15) | copy-start | bytes 8257540
  78.7 4.4 %copy-start.2 = (bf16[1,896,1536]{2,1,0:T(8,128)(2,1)S(1)}, bf16[1,896,1536]{2,1,0:T(8,128)(2,1)}, u32[]{:S(2)}) copy-start(bf16[1,896,1536]{2,1,0:T(8,128)(2,1)} %param.14) | copy-start | bytes 8257540

commit v2 on v1

v2 whole, which is shorter than its diff:
```python
import functools

import jax
import jax.numpy as jnp
from jax import lax
from jax.experimental import pallas as pl
from jax.experimental.pallas import tpu as pltpu
from jax.sharding import PartitionSpec as P

MESH = pl.DeviceIdType.MESH
LANES = 128
SUBLANES = 8


def silu_parts(pre_act):
    logistic = jax.nn.sigmoid(pre_act)
    return (pre_act * logistic, logistic * (1.0 + pre_act * (1.0 - logistic)))


def flip(index, mask):
    bit = 1
    while bit <= mask:
        if mask & bit:
            index = index + bit * (1 - 2 * lax.rem(lax.div(index, bit), 2))
        bit *= 2
    return index


class Copies:
    def __init__(self, send_sem, recv_sem):
        self.send_sem, self.recv_sem, self.made = send_sem, recv_sem, []

    def start(self, src, dst, device):
        at = len(self.made)
        copy = pltpu.make_async_remote_copy(
            src_ref=src,
            dst_ref=dst,
            send_sem=self.send_sem.at[at],
            recv_sem=self.recv_sem.at[at],
            device_id=device,
            device_id_type=MESH,
        )
        copy.start()
        self.made.append(copy)
        return copy


def greet(peers):
    barrier = pltpu.get_barrier_semaphore()
    for peer in peers:
        pl.semaphore_signal(barrier, inc=1, device_id=peer, device_id_type=MESH)
    pl.semaphore_wait(barrier, len(peers))


def copy_count(columns, experts, cores):
    probe = columns * cores + experts
    if columns == 4:
        per_block = 6 + 7 * (cores - 1)
        return (experts - 1) * 2 + (columns - 1) + experts * per_block + probe
    return (experts - 1) * 2 + (columns - 1) * 2 + columns * (cores - 1) + probe


def row_tile(rows):
    return max(tile for tile in range(16, 257, 16) if rows % tile == 0)


def moe_kernel(
    columns,
    experts,
    cores,
    rows_ref,
    probs_ref,
    weight_hbm,
    gate_hbm,
    up_hbm,
    ups_ref,
    acc_ref,
    probs_out,
    probe_out,
    gathered,
    weight_ref,
    gate_ref,
    up_ref,
    hidden_ref,
    weighted_ref,
    part_ref,
    first,
    total,
    second,
    load_sem,
    send_sem,
    recv_sem,
):
    d, e, t = lax.axis_index("dp"), lax.axis_index("expert"), lax.axis_index("tensor")
    capacity, half = rows_ref.shape[1], rows_ref.shape[2]
    group_size = experts * capacity
    units = weight_ref.shape[0]
    tile = row_tile(units)
    tiles = units // tile
    loads = [
        pltpu.make_async_copy(src, dst, load_sem.at[at])
        for at, (src, dst) in enumerate(
            ((gate_hbm, gate_ref), (up_hbm, up_ref), (weight_hbm, weight_ref))
        )
    ]
    for load in loads:
        load.start()
    greet(
        [(d, flip(e, k), t) for k in range(1, experts)]
        + [
            (flip(d, m), e, flip(t, f))
            for m in range(columns)
            for f in range(cores)
            if m or f
        ]
    )
    copies = Copies(send_sem, recv_sem)
    base = pl.multiple_of(t * half, half)
    mine = pl.ds(base, half)
    along, small = [None], [None]
    for k in range(1, experts):
        to = (d, flip(e, k), t)
        along.append(copies.start(rows_ref.at[flip(e, k)], gathered.at[d, e, :, mine], to))
        small.append(copies.start(probs_ref.at[flip(e, k)], probs_out.at[d, e], to))
    last = [[] for _ in range(columns)]

    def to_cores(m, src, dst):
        for f in range(1, cores):
            last[m].append(copies.start(src, dst, (d, e, flip(t, f))))

    def make_hidden(at):
        if at == 0:
            loads[0].wait()
            loads[1].wait()
        span = pl.ds(at * tile, tile)
        gate = gate_ref[span, :].astype(jnp.float32)
        hidden_ref[span, :] = (gate * jax.nn.sigmoid(gate) * up_ref[span, :].astype(jnp.float32)).astype(
            jnp.bfloat16
        )

    def some_hidden(k):
        for at in range(k * tiles // experts, (k + 1) * tiles // experts):
            make_hidden(at)

    def spread_probs():
        for k in range(1, experts):
            small[k].wait_recv()
        group = probs_out.at[d]
        for m in range(1, columns):
            last[m].append(copies.start(group, group, (flip(d, m), e, t)))

    firsts = {}

    def compute(m):
        for copy in last[m]:
            copy.wait_recv()
        where = flip(d, m)
        cols = pl.ds(pl.multiple_of(where * group_size, 128), group_size)
        eye = lax.broadcasted_iota(jnp.int32, (capacity, capacity), 0) == lax.broadcasted_iota(
            jnp.int32, (capacity, capacity), 1
        )
        for j in range(experts):
            prob = probs_out[where, j][0:1, 0:capacity]
            diag = jnp.where(eye, prob, 0.0).astype(jnp.bfloat16)
            weighted_ref[pl.ds(j * capacity, capacity), :] = jnp.dot(
                diag, gathered[where, j], preferred_element_type=jnp.float32
            ).astype(jnp.bfloat16)

        def up_step(i, part):
            span = pl.ds(pl.multiple_of(i * tile, tile), tile)
            block = gathered[where].reshape(group_size, half * cores)
            ups = lax.dot_general(
                weight_ref[span, :], block, (((1,), (1,)), ((), ())),
                preferred_element_type=jnp.float32,
            )
            ups_ref[span, cols] = ups
            value = ups * hidden_ref[span, cols].astype(jnp.float32)
            return part + jnp.sum(value, axis=0, keepdims=True)

        part = lax.fori_loop(0, tiles, up_step, jnp.zeros((1, group_size), jnp.float32))
        part_ref[where] = jnp.broadcast_to(part, (8, group_size))
        for f in range(cores):
            if m or f:
                at = m * cores + f - 1
                firsts[at] = copies.start(
                    part_ref.at[where], first.at[at], (where, e, flip(t, f))
                )

        def down_step(i, carry):
            span = pl.ds(pl.multiple_of(i * tile, tile), tile)
            out = jnp.dot(
                hidden_ref[span, cols], weighted_ref[...], preferred_element_type=jnp.float32
            )
            acc_ref[span, :] = out if m == 0 else acc_ref[span, :] + out
            return carry

        lax.fori_loop(0, tiles, down_step, 0)

    if columns == 4:
        piece = half // 2
        cuts = [pl.ds(pl.multiple_of(base + p * piece, piece), piece) for p in range(2)]
        sent = {}

        def spread(k):
            origin = flip(e, k)
            if k > 0:
                along[k].wait_recv()
            for m, order in ((1, (0, 1)), (2, (1, 0))):
                for p in order:
                    here = gathered.at[d, origin, :, cuts[p]]
                    src = rows_ref.at[e, :, pl.ds(p * piece, piece)] if k == 0 else here
                    sent[k, m, p] = copies.start(src, here, (flip(d, m), e, t))
            whole = gathered.at[d, origin, :, mine]
            to_cores(0, rows_ref.at[e] if k == 0 else whole, whole)

        def forward(k):
            origin = flip(e, k)
            for m, p in ((1, 0), (2, 1)):
                sent[k, m, p].wait_recv()
                block = gathered.at[flip(d, m), origin, :, cuts[p]]
                sent[k, 3, p] = copies.start(block, block, (flip(d, 3 - m), e, t))
                to_cores(m, block, block)
            for m, p in ((1, 1), (2, 0)):
                sent[k, m, p].wait_recv()
                block = gathered.at[flip(d, m), origin, :, cuts[p]]
                to_cores(m, block, block)

        def finish(k):
            for p in range(2):
                sent[k, 3, p].wait_recv()
                block = gathered.at[flip(d, 3), flip(e, k), :, cuts[p]]
                to_cores(3, block, block)

        spread(0)
        gathered[d, e, :, mine] = rows_ref[e]
        probs_out[d, e] = probs_ref[e]
        some_hidden(0)
        for k in range(1, experts):
            spread(k)
            some_hidden(k)
            if k == 1:
                forward(0)
        spread_probs()
        for k in range(1, experts - 1):
            forward(k)
        loads[2].wait()
        compute(0)
        forward(experts - 1)
        compute(1)
        for k in range(experts - 1):
            finish(k)
        compute(2)
        finish(experts - 1)
        compute(3)
    else:
        gathered[d, e, :, mine] = rows_ref[e]
        probs_out[d, e] = probs_ref[e]
        for k in range(1, experts):
            along[k].wait_recv()
        group = gathered.at[d, :, :, mine]
        spreads = [copies.start(group, group, (flip(d, m), e, t)) for m in range(1, columns)]
        to_cores(0, group, group)
        spread_probs()
        for at in range(tiles):
            make_hidden(at)
        loads[2].wait()
        compute(0)
        for m in range(1, columns):
            spreads[m - 1].wait_recv()
            block = gathered.at[flip(d, m), :, :, mine]
            to_cores(m, block, block)
            compute(m)
    acc = part_ref[d]
    for at in range(columns * cores - 1):
        firsts[at].wait_recv()
        acc = acc + first[at]
    total[...] = acc
    backs = [copies.start(total, second.at[k - 1], (d, flip(e, k), t)) for k in range(1, experts)]
    probe_out[e] = acc
    for k in range(1, experts):
        backs[k - 1].wait_recv()
        probe_out[flip(e, k)] = second[k - 1]
    for copy in copies.made:
        copy.wait_send()


def local(out_grad, seq_ids, seq_weights, expert_ids, route_probs, down_weight, gate_pre, up_pre):
    experts = lax.axis_size("expert")
    columns = lax.axis_size("dp")
    cores = lax.axis_size("tensor")
    token_count = seq_ids.shape[1]
    slots = gate_pre.shape[2]
    capacity = slots // (columns * experts)
    half_width = out_grad.shape[1]
    width = half_width * cores
    seq_count = seq_weights.shape[1]
    block_size = experts * capacity
    padded = -(-capacity // LANES) * LANES
    gate_local = gate_pre[0]
    up_local = up_pre[0]
    weight_local = down_weight[0]
    member = (seq_ids[0][:, None] == jnp.arange(seq_count, dtype=jnp.int32)[None, :]).astype(
        jnp.float32
    )
    weight_tok = jnp.sum(member * seq_weights[0][None, :], axis=1)
    scaled = (weight_tok[:, None] * out_grad.astype(jnp.float32)).astype(jnp.bfloat16)
    chosen = expert_ids.reshape(-1)
    pairs = chosen.shape[0]
    onehot = chosen[:, None] == jnp.arange(experts, dtype=jnp.int32)[None, :]
    rank = jnp.arange(pairs, dtype=jnp.int32)
    lower = (rank[None, :] < rank[:, None]).astype(jnp.bfloat16)
    earlier = jnp.dot(lower, onehot.astype(jnp.bfloat16), preferred_element_type=jnp.float32)
    position = jnp.sum(jnp.where(onehot, earlier, 0.0), axis=1).astype(jnp.int32)
    slot_index = chosen * capacity + position
    filled = slot_index[None, :] == jnp.arange(block_size, dtype=jnp.int32)[:, None]
    send_probs = jnp.sum(
        jnp.where(filled, route_probs.reshape(-1).astype(jnp.float32)[None, :], 0.0), axis=1
    )
    by_token = slot_index.reshape(token_count, 2)
    every = jnp.arange(block_size, dtype=jnp.int32)[:, None]
    picks = ((by_token[:, 0][None, :] == every) | (by_token[:, 1][None, :] == every)).astype(
        jnp.bfloat16
    )
    send_rows = jnp.dot(picks, scaled, preferred_element_type=jnp.float32).astype(jnp.bfloat16)
    prob_tile = jnp.zeros((experts, SUBLANES, padded), jnp.float32)
    prob_tile = prob_tile + jnp.pad(
        send_probs.reshape(experts, 1, capacity), ((0, 0), (0, 0), (0, padded - capacity))
    )
    amount = copy_count(columns, experts, cores)
    units = weight_local.shape[0]
    anywhere = pl.BlockSpec(memory_space=pl.ANY)
    inside = pl.BlockSpec(memory_space=pltpu.VMEM)
    upstream, grad_w, probs_all, probes = pl.pallas_call(
        functools.partial(moe_kernel, columns, experts, cores),
        out_shape=(
            jax.ShapeDtypeStruct((units, slots), jnp.float32),
            jax.ShapeDtypeStruct((units, width), jnp.float32),
            jax.ShapeDtypeStruct((columns, experts, SUBLANES, padded), jnp.float32),
            jax.ShapeDtypeStruct((experts, SUBLANES, block_size), jnp.float32),
        ),
        in_specs=[inside, inside, anywhere, anywhere, anywhere],
        out_specs=[inside] * 4,
        scratch_shapes=[
            pltpu.VMEM((columns, experts, capacity, width), jnp.bfloat16),
            pltpu.VMEM((units, width), jnp.bfloat16),
            pltpu.VMEM((units, slots), jnp.bfloat16),
            pltpu.VMEM((units, slots), jnp.bfloat16),
            pltpu.VMEM((units, slots), jnp.bfloat16),
            pltpu.VMEM((block_size, width), jnp.bfloat16),
            pltpu.VMEM((columns, SUBLANES, block_size), jnp.float32),
            pltpu.VMEM((columns * cores - 1, SUBLANES, block_size), jnp.float32),
            pltpu.VMEM((SUBLANES, block_size), jnp.float32),
            pltpu.VMEM((experts - 1, SUBLANES, block_size), jnp.float32),
            pltpu.SemaphoreType.DMA((3,)),
            pltpu.SemaphoreType.DMA((amount,)),
            pltpu.SemaphoreType.DMA((amount,)),
        ],
        compiler_params=pltpu.CompilerParams(
            collective_id=0, has_side_effects=True, vmem_limit_bytes=50 * 1024 * 1024
        ),
        name="moe",
    )(send_rows.reshape(experts, capacity, half_width), prob_tile, weight_local, gate_local, up_local)
    arrived_probs = probs_all[:, :, 0, :capacity].reshape(slots)
    gate_piece = gate_local.astype(jnp.float32)
    up_piece = up_local.astype(jnp.float32)
    activated, derivative = silu_parts(gate_piece)
    grad_hidden = arrived_probs[None, :] * upstream
    gate_out = (grad_hidden * up_piece * derivative).astype(jnp.bfloat16)
    up_out = (grad_hidden * activated).astype(jnp.bfloat16)
    grad_w = grad_w.astype(jnp.bfloat16)
    own = lax.dynamic_slice_in_dim(
        probes[:, 0, :], lax.axis_index("expert") * capacity, capacity, 1
    )
    returned = own.reshape(-1)
    grad_probs = jnp.sum(jnp.where(filled, returned[:, None], 0.0), axis=0).reshape(token_count, 2)
    return (gate_out[None], up_out[None], grad_w[None], grad_probs)


def solution(mesh):
    return jax.shard_map(
        local,
        mesh=mesh,
        in_specs=(
            P(("dp", "expert"), "tensor"),
            P(("dp", "expert"), None),
            P(("dp", "expert"), None),
            P(("dp", "expert"), None),
            P(("dp", "expert"), None),
            P("expert", ("dp", "tensor"), None),
            P("expert", ("dp", "tensor"), None),
            P("expert", ("dp", "tensor"), None),
        ),
        out_specs=(
            P("expert", ("dp", "tensor"), None),
            P("expert", ("dp", "tensor"), None),
            P("expert", ("dp", "tensor"), None),
            P(("dp", "expert"), None),
        ),
        check_vma=False,
    )
```

time: 91.3 us -> 88.7 us (0.972)
  matrix products: 24.2 us -> 1.59 us
  Pallas kernels: 52.7 us -> 65.8 us
  other arithmetic: 5.77 us -> 13.9 us
  local copies, waits for them, and re-layouts: 7.53 us -> 6.4 us
    dot_general x2 -> x0, matrix products: 22.7 us -> none  [the longest x1 14.8 us: local(): lax.dot_general(weight_local, gathered, (((1,), (1,)), ((), ())), preferr...]
    pallas_call x2 -> x1, Pallas kernels: 52.7 us -> 65.8 us  [local(): pl.pallas_call(functools.partial(moe_kernel, columns, experts, cores), ou...]
    broadcast_in_dim x0 -> x2, other arithmetic: none -> 12.1 us  [local(): return (gate_out[None], up_out[None], grad_w[None], grad_probs)]
    convert_element_type x1 -> x0, other arithmetic: 4.01 us -> none  [local(): (arrived_probs[:, None] * gathered.astype(jnp.float32)).astype(jnp.bfloat16)]
where the time goes in v2:
time: 88.7 us; the launch traced here: 88.4 us
  Pallas kernels  65.8 us (74%)
  other arithmetic  13.9 us (16%)
  local copies, waits for them, and re-layouts  6.4 us (7%)
  matrix products  1.59 us (2%)
    pallas_call x1, Pallas kernels, local(): pl.pallas_call(functools.partial(moe_kernel, columns, experts, cores), ou...  65.8 us
    broadcast_in_dim x2, other arithmetic, local(): return (gate_out[None], up_out[None], grad_w[None], grad_probs)  12.1 us
    unnamed x8, local copies, waits for them, and re-layouts  3.82 us

profile of v2, /device:TPU:0, one launch (start us, length us, event | category | flops | bytes accessed | tf_op | source)
XLA Modules:
  0.0 88.4 jit_solution(43580929101400311)
XLA Ops:
  0.6 0.8 copy.27
  1.4 0.1 eq.73
  1.6 0.2 fusion.11
  1.8 0.1 convert_element_type.52
  1.9 0.1 copy.28
  2.0 0.7 multiply_add_fusion.1
  2.7 0.8 select_reduce_fusion.2
  3.4 1.4 %convolution_convert_fusion = bf16[384,1024]{1,0:T(8,128)(2,1)S(1)} fusion(bf16[128,1024]{1,0:T(8,128)(2,1)} %param.8, f32[128]{0:T(128)S(1)} %select_reduce_fusion.2, s32[128]{0:T(128)S(1)} %get-tuple-element.31, s32[128]{0:T(128)S(1)} %get-tuple-element.30), kind=kOutput, calls=%fused_computation.15 | convolution fusion | flops 101597184 | bytes 1050112 | tf_op jit(solution)/shard_map/dot_general | solution.py:324
  4.9 0.8 copy.29
  5.6 0.1 reshape.50
  5.8 0.2 select_reduce_fusion.1
  5.9 0.1 reshape.48
  6.0 0.0 copy-start
  6.0 1.8 %copy-done = bf16[1,896,1536]{2,1,0:T(8,128)(2,1)S(1)} copy-done((bf16[1,896,1536]{2,1,0:T(8,128)(2,1)S(1)}, bf16[1,896,1536]{2,1,0:T(8,128)(2,1)}, u32[]{:S(2)}) %copy-start) | copy-done | bytes 2752536
  7.8 0.0 copy-start.1
  7.8 65.8 %moe.1 = (f32[896,1536]{1,0:T(8,128)}, f32[896,2048]{1,0:T(8,128)}, f32[4,4,8,128]{3,2,1,0:T(8,128)S(1)}, f32[4,8,384]{2,1,0:T(8,128)S(1)}) custom-call(bf16[4,96,1024]{2,1,0:T(8,128)(2,1)S(1)} %bitcast.22, f32[4,8,128]{2,1,0:T(8,128)S(1)} %add.31.probs_ref, bf16[896,2048]{1,0:T(8,128)(2,1)} %bitcast.24, bf16[896,1536]{1,0:T(8,128)(2,1)S(1)} %bitcast.21, ...), custom_call_target="tpu_custom_call" | custom-call | tf_op jit(solution)/shard_map/moe/pallas_call | solution.py:333
  73.6 0.0 copy-start.2
  73.7 0.6 copy-done.2
  74.3 0.1 mul.73
  74.4 0.0 copy-done.1
  74.4 6.6 %fusion.9 = (bf16[1,896,1536]{2,1,0:T(8,128)(2,1)}, bf16[1,896,1536]{2,1,0:T(8,128)(2,1)}) fusion(f32[896,1536]{1,0:T(8,128)} %get-tuple-element.9, f32[1536]{0:T(1024)S(1)} %mul.73, bf16[1,896,1536]{2,1,0:T(8,128)(2,1)S(1)} %copy-done.1, bf16[1,896,1536]{2,1,0:T(8,128)(2,1)} %param.15), kind=kLoop, calls=%fused_computation.13 | loop fusion | flops 22020096 | bytes 16521216 | tf_op jit(solution)/shard_map/broadcast_in_dim | solution.py:376
  81.0 0.8 slice.15
  81.8 0.1 dynamic-slice_reduce_fusion
  81.9 0.1 broadcast_in_dim.52
  82.0 0.1 select_reduce_fusion
  82.1 0.1 reshape.49
  82.3 0.6 copy.30
  82.9 5.5 %convert_bitcast_fusion = bf16[1,896,2048]{2,1,0:T(8,128)(2,1)} fusion(f32[896,2048]{1,0:T(8,128)} %get-tuple-element.10), kind=kLoop, calls=%fused_computation.12 | loop fusion | flops 1835008 | bytes 11010048 | tf_op jit(solution)/shard_map/broadcast_in_dim | solution.py:376
  (6 shorter events, 0.1 us)
Async XLA Ops:
  6.0 1.8 %copy-start = (bf16[1,896,1536]{2,1,0:T(8,128)(2,1)S(1)}, bf16[1,896,1536]{2,1,0:T(8,128)(2,1)}, u32[]{:S(2)}) copy-start(bf16[1,896,1536]{2,1,0:T(8,128)(2,1)} %param.14) | copy-start | bytes 8257540
  7.8 66.6 %copy-start.1 = (bf16[1,896,1536]{2,1,0:T(8,128)(2,1)S(1)}, bf16[1,896,1536]{2,1,0:T(8,128)(2,1)}, u32[]{:S(2)}) copy-start(bf16[1,896,1536]{2,1,0:T(8,128)(2,1)} %param.14) | copy-start | bytes 8257540
  73.6 0.6 copy-start.2
